TPU v7x, 32 devices: a whole 2x2x4 slice. The times are simulated.
32 devices in a mesh: bins: 4 (over x, core), sta: 8 (over z, y).
Axes of the slice: x: 2, y: 2, z: 4, core: 2. Of those that a mesh axis runs over, the one named last changes fastest.
Arguments:
- spectra: bfloat16 [2, 128, 8, 2048], P(None, 'bins', None, 'sta'), may hold values from -110 to 110
- coords: int32 [2, 2048], replicated, may hold values from 0 to 2047
- slowness: int32 [2, 2048], replicated, may hold values from -32 to 31
Outputs:
- beam_power: float32 [128, 2048], P('bins', 'sta')
All inputs are finite; a program needn't handle non-finite values.
Results may differ from a plain program's by a relative error of at most 0.002.
Values may be sent and summed in bfloat16 or wider, within the bound.
A program may use at most 64 MiB of HBM per device.

v0:
```python
import functools
import math

import jax
import jax.numpy as jnp
from jax import lax
from jax.experimental import pallas as pl
from jax.experimental.pallas import tpu as pltpu
from jax.sharding import PartitionSpec as P

epsilon = 1e-06
MESH = pl.DeviceIdType.MESH

SIN_COEFS = (6.28318501, -41.3415909, 81.5999451, -76.6144714, 41.3428841, -12.4712439)
COS_COEFS = (1.0, -19.7392044, 64.9391174, -85.4501419, 60.1676292, -25.9675999, 6.52865839)


def horner(coefs, z):
    acc = jnp.full_like(z, coefs[-1])
    for c in coefs[-2::-1]:
        acc = acc * z + c
    return acc


def cos_sin(index):
    turns = (index << 11).astype(jnp.float32) * (2.0 ** -32)
    z = turns * turns
    return horner(COS_COEFS, z), horner(SIN_COEFS, z) * turns


def kernel(
    dims,
    spectra,
    coords_hbm,
    slowness_hbm,
    out,
    coords,
    slowness,
    own,
    blocks,
    squares,
    scales,
    cos_b,
    sin_b,
    rotor,
    right,
    left,
    product,
    grid_hi_lo,
    onehot,
    picked,
    returned,
    own_sem,
    local_sem,
    coords_sem,
    slow_sem,
    sq_send,
    sq_recv,
    sc_send,
    sc_recv,
    bl_send,
    bl_recv,
    re_send,
    re_recv,
):
    n_bins, n_sta, groups, copies, fb, bins_dev, segs, sta_dev, beams_dev = dims
    me = lax.axis_index("sta")
    mb = lax.axis_index("bins")
    group = me // copies
    lane_of = me % copies
    f32, bf16 = jnp.float32, jnp.bfloat16

    def partner(o):
        if n_sta & (n_sta - 1):
            return (me + o) % n_sta
        return me ^ o

    def origin(o):
        if n_sta & (n_sta - 1):
            return (me - o + n_sta) % n_sta
        return me ^ o

    own_copy = pltpu.make_async_copy(spectra, own, own_sem)
    own_copy.start()
    local_copy = pltpu.make_async_copy(
        spectra.at[:, pl.ds(group * fb, fb)], blocks.at[me], local_sem
    )
    local_copy.start()
    coords_copy = pltpu.make_async_copy(coords_hbm, coords, coords_sem)
    coords_copy.start()
    slow_copy = pltpu.make_async_copy(slowness_hbm, slowness, slow_sem)
    slow_copy.start()

    barrier = pltpu.get_barrier_semaphore()
    for o in range(1, n_bins):
        pl.semaphore_signal(
            barrier, inc=1, device_id={"bins": (mb + o) % n_bins}, device_id_type=MESH
        )
    for o in range(1, n_sta):
        pl.semaphore_signal(
            barrier, inc=1, device_id={"sta": partner(o)}, device_id_type=MESH
        )

    own_copy.wait()

    def square_step(f, acc):
        re = own[0, f].astype(f32)
        im = own[1, f].astype(f32)
        return acc + re * re + im * im

    squares[mb] = lax.fori_loop(
        0, bins_dev, square_step, jnp.zeros((segs, sta_dev), f32), unroll=True
    )

    coords_copy.wait()
    first_bin = mb * bins_dev + group * fb + 1

    def table_step(step, carry):
        f = step // n_sta
        at = pl.ds(pl.multiple_of((step % n_sta) * sta_dev, sta_dev), sta_dev)
        bin_number = first_bin + f
        east = coords[0:1, at] * bin_number
        north = coords[1:2, at] * bin_number
        ids = lax.broadcasted_iota(jnp.int32, (8, sta_dev), 0)
        cb, sb = cos_sin((2 * ids + 1) * east)
        cos_b[f, :, at] = cb
        sin_b[f, :, at] = sb
        steps = jnp.where(ids == 0, 16, jnp.where(ids == 1, 48, 1))
        ca, sa = cos_sin(steps * east + jnp.where(ids == 2, north, 0))
        rotor[f, 0, :, at] = ca
        rotor[f, 1, :, at] = sa
        ids = lax.broadcasted_iota(jnp.int32, (16, sta_dev), 0)
        for half in range(2):
            cy, sy = cos_sin((2 * ids + (32 * half + 1)) * north)
            for a in range(2):
                c, s = ca[a : a + 1], sa[a : a + 1]
                cc, ss, sc, cs = c * cy, s * sy, s * cy, c * sy
                base = a * 64 + half * 16
                right[f, base : base + 16, at] = (cc - ss).astype(bf16)
                right[f, base + 32 : base + 48, at] = (cc + ss).astype(bf16)
                right[f, base + 128 : base + 144, at] = (sc + cs).astype(bf16)
                right[f, base + 160 : base + 176, at] = (sc - cs).astype(bf16)
        return carry

    lax.fori_loop(0, fb * n_sta // 2, table_step, 0)
    product[...] = jnp.zeros_like(product)

    slow_copy.wait()
    sx = slowness[0:1, :] + 32
    sy = slowness[1:2, :] + 32
    a_index = sx // 16
    flipped = a_index < 2
    y_index = jnp.where(flipped, 63 - sy, sy)
    y_slot = jnp.where(y_index >= 32, y_index - 32, 63 - y_index)
    a_slot = jnp.where(flipped, 1 - a_index, a_index - 2)
    column = jnp.where(flipped, 128, 0) + a_slot * 64 + y_slot
    for i in range(16):
        ids = lax.broadcasted_iota(jnp.int32, (16, column.shape[1]), 0) + 16 * i
        onehot[i * 16 : (i + 1) * 16, :] = jnp.where(ids == column, 1.0, 0.0).astype(bf16)

    pl.semaphore_wait(barrier, n_bins + n_sta - 2)

    def square_send(o):
        return pltpu.make_async_remote_copy(
            src_ref=squares.at[mb],
            dst_ref=squares.at[mb],
            send_sem=sq_send.at[o],
            recv_sem=sq_recv.at[mb],
            device_id={"bins": (mb + o) % n_bins},
            device_id_type=MESH,
        )

    def square_arrival(o):
        source = (mb + o) % n_bins
        return pltpu.make_async_remote_copy(
            src_ref=squares.at[source],
            dst_ref=squares.at[source],
            send_sem=sq_send.at[o],
            recv_sem=sq_recv.at[source],
            device_id={"bins": source},
            device_id_type=MESH,
        )

    def scale_send(o):
        return pltpu.make_async_remote_copy(
            src_ref=scales.at[me],
            dst_ref=scales.at[me],
            send_sem=sc_send.at[o],
            recv_sem=sc_recv.at[me],
            device_id={"sta": partner(o)},
            device_id_type=MESH,
        )

    def scale_arrival(o):
        source = origin(o)
        return pltpu.make_async_remote_copy(
            src_ref=scales.at[source],
            dst_ref=scales.at[source],
            send_sem=sc_send.at[o],
            recv_sem=sc_recv.at[source],
            device_id={"sta": source},
            device_id_type=MESH,
        )

    def block_send(o):
        target = partner(o)
        return pltpu.make_async_remote_copy(
            src_ref=own.at[:, pl.ds((target // copies) * fb, fb)],
            dst_ref=blocks.at[me],
            send_sem=bl_send.at[o],
            recv_sem=bl_recv.at[me],
            device_id={"sta": target},
            device_id_type=MESH,
        )

    def block_arrival(o):
        source = origin(o)
        return pltpu.make_async_remote_copy(
            src_ref=blocks.at[source],
            dst_ref=blocks.at[source],
            send_sem=bl_send.at[o],
            recv_sem=bl_recv.at[source],
            device_id={"sta": source},
            device_id_type=MESH,
        )

    for o in range(1, n_bins):
        square_send(o).start()
    for o in range(n_sta - 1, 0, -1):
        block_send(o).start()

    lax.fori_loop(fb * n_sta // 2, fb * n_sta, table_step, 0)
    for o in range(1, n_bins):
        square_arrival(o).wait_recv()
    total = squares[0]
    for b in range(1, n_bins):
        total = total + squares[b]
    scales[me] = 1.0 / jnp.sqrt(total / (2 * bins_dev * n_bins) + epsilon)
    for o in range(1, n_sta):
        scale_send(o).start()

    local_copy.wait()

    def fill(o, source):
        at = pl.ds(pl.multiple_of(source * sta_dev, sta_dev), sta_dev)
        inverse = scales[source]
        for f in range(fb):
            re = (blocks[source, 0, f].astype(f32) * inverse).astype(bf16).astype(f32)
            im = (blocks[source, 1, f].astype(f32) * inverse).astype(bf16).astype(f32)
            c0 = rotor[f, 0, 2:3, at]
            s0 = rotor[f, 1, 2:3, at]
            parts = (re * c0 - im * s0, im * c0 + re * s0)
            trig = (cos_b[f, :, at], sin_b[f, :, at])
            for p in range(2):
                for ri in range(2):
                    for g in range(0, segs, 2):
                        both = jnp.concatenate(
                            [parts[ri][g : g + 1] * trig[p], parts[ri][g + 1 : g + 2] * trig[p]], 0
                        )
                        base = ((p * 2 + ri) * segs + g) * 8
                        left[f, base : base + 16, :] = both.astype(bf16)
            product[f] += lax.dot_general(
                left[f], right[f, :, at], (((1,), (1,)), ((), ())), preferred_element_type=f32
            )

    def arrive_step(o, carry):
        @pl.when(o > 0)
        def _():
            block_arrival(o).wait_recv()
            scale_arrival(o).wait_recv()

        fill(o, origin(o))
        return carry

    lax.fori_loop(0, n_sta, arrive_step, 0)

    part = segs * 8

    def bin_power(f, carry):
        sums = [None] * 4
        for g in range(segs):
            r0 = g * 8
            ccr, csr = product[f, r0 : r0 + 8, :128], product[f, r0 : r0 + 8, 128:]
            r0 += part
            cci, csi = product[f, r0 : r0 + 8, :128], product[f, r0 : r0 + 8, 128:]
            r0 += part
            scr, ssr = product[f, r0 : r0 + 8, :128], product[f, r0 : r0 + 8, 128:]
            r0 += part
            sci, ssi = product[f, r0 : r0 + 8, :128], product[f, r0 : r0 + 8, 128:]
            pr, pi, mr, mi = ccr - ssr, cci - ssi, ccr + ssr, cci + ssi
            tr, ti, dr, di = scr + csr, sci + csi, scr - csr, sci - csi
            amps = (
                (pr + ti, pi - tr),
                (mr + di, mi - dr),
                (mr - di, mi + dr),
                (pr - ti, pi + tr),
            )
            for c, (x, y) in enumerate(amps):
                power = x * x + y * y
                sums[c] = power if sums[c] is None else sums[c] + power
        grid = jnp.concatenate(
            [jnp.concatenate(sums[0:2], 1), jnp.concatenate(sums[2:4], 1)], 0
        )
        hi = grid.astype(bf16)
        lo = (grid - hi.astype(f32)).astype(bf16)
        grid_hi_lo[0, f] = hi
        grid_hi_lo[1, f] = lo
        return carry

    lax.fori_loop(0, fb, bin_power, 0)

    norm = 1.0 / (n_sta * sta_dev * segs)
    rows = jnp.concatenate(
        [grid_hi_lo[h, f] for h in range(2) for f in range(fb)], 0
    )

    def result_send(o):
        target = ((group + o) % groups) * copies + lane_of
        return pltpu.make_async_remote_copy(
            src_ref=picked.at[target],
            dst_ref=returned.at[group],
            send_sem=re_send.at[o],
            recv_sem=re_recv.at[group],
            device_id={"sta": target},
            device_id_type=MESH,
        )

    def result_arrival(o):
        source = (group + o) % groups
        return pltpu.make_async_remote_copy(
            src_ref=returned.at[source],
            dst_ref=returned.at[source],
            send_sem=re_send.at[o],
            recv_sem=re_recv.at[source],
            device_id={"sta": source * copies + lane_of},
            device_id_type=MESH,
        )

    ids16 = lax.broadcasted_iota(jnp.int32, (16, beams_dev), 0)
    packed_rows = 16 * fb
    place = returned.at[group]
    for o in list(range(1, groups)) + [0]:
        target = ((group + o) % groups) * copies + lane_of
        at = pl.ds(pl.multiple_of(target * beams_dev, beams_dev), beams_dev)
        values = jnp.dot(rows, onehot[:, at], preferred_element_type=f32)
        values = values[:packed_rows] + values[packed_rows:]
        sx_at = slowness[0:1, at] + 32
        b_at = sx_at % 16
        row_at = jnp.where(b_at >= 8, b_at - 8, 15 - b_at)
        keep = jnp.where(ids16 == row_at, norm, 0.0)
        for f in range(fb):
            line = jnp.sum(values[f * 16 : (f + 1) * 16] * keep, axis=0, keepdims=True)
            if o:
                picked[target, f : f + 1, :] = line
            else:
                place[f : f + 1, :] = line
        if o:
            result_send(o).start()

    for o in range(1, groups):
        result_arrival(o).wait_recv()
    for g in range(groups):
        out[g * fb : (g + 1) * fb, :] = returned[g]

    for o in range(1, n_bins):
        square_send(o).wait_send()
    for o in range(1, n_sta):
        block_send(o).wait_send()
        scale_send(o).wait_send()
    for o in range(1, groups):
        result_send(o).wait_send()


def solution(mesh):
    n_bins, n_sta = mesh.shape["bins"], mesh.shape["sta"]

    def local(spectra, coords, slowness):
        _, bins_dev, segs, sta_dev = spectra.shape
        stations, beams = coords.shape[1], slowness.shape[1]
        beams_dev = beams // n_sta
        groups = math.gcd(bins_dev, n_sta)
        copies = n_sta // groups
        fb = bins_dev // groups
        dims = (n_bins, n_sta, groups, copies, fb, bins_dev, segs, sta_dev, beams_dev)
        f32, bf16 = jnp.float32, jnp.bfloat16
        dma = pltpu.SemaphoreType.DMA
        return pl.pallas_call(
            functools.partial(kernel, dims),
            out_shape=pltpu.VMEM((bins_dev, beams_dev), f32),
            in_specs=[
                pl.BlockSpec(memory_space=pltpu.HBM),
                pl.BlockSpec(memory_space=pltpu.HBM),
                pl.BlockSpec(memory_space=pltpu.HBM),
            ],
            out_specs=pl.BlockSpec(memory_space=pltpu.VMEM),
            scratch_shapes=[
                pltpu.VMEM((2, stations), jnp.int32),
                pltpu.VMEM((2, beams), jnp.int32),
                pltpu.VMEM((2, bins_dev, segs, sta_dev), bf16),
                pltpu.VMEM((n_sta, 2, fb, segs, sta_dev), bf16),
                pltpu.VMEM((n_bins, segs, sta_dev), f32),
                pltpu.VMEM((n_sta, segs, sta_dev), f32),
                pltpu.VMEM((fb, 8, stations), f32),
                pltpu.VMEM((fb, 8, stations), f32),
                pltpu.VMEM((fb, 2, 8, stations), f32),
                pltpu.VMEM((fb, 256, stations), bf16),
                pltpu.VMEM((fb, 32 * segs, sta_dev), bf16),
                pltpu.VMEM((fb, 32 * segs, 256), f32),
                pltpu.VMEM((2, fb, 16, 256), bf16),
                pltpu.VMEM((256, beams), bf16),
                pltpu.VMEM((n_sta, fb, beams_dev), f32),
                pltpu.VMEM((groups, fb, beams_dev), f32),
                dma,
                dma,
                dma,
                dma,
                dma((n_bins,)),
                dma((n_bins,)),
                dma((n_sta,)),
                dma((n_sta,)),
                dma((n_sta,)),
                dma((n_sta,)),
                dma((groups,)),
                dma((groups,)),
            ],
            compiler_params=pltpu.CompilerParams(
                collective_id=0,
                has_side_effects=True,
                vmem_limit_bytes=33554432,
            ),
            name="beam_power",
        )(*(pltpu.with_memory_space_constraint(x, pltpu.HBM) for x in (spectra, coords, slowness)))

    in_specs = (P(None, "bins", None, "sta"), P(), P())
    out_specs = P("bins", "sta")
    return jax.shard_map(local, mesh=mesh, in_specs=in_specs, out_specs=out_specs, check_vma=False)
```

profile of v0, /device:TPU:0, one launch (start us, length us, event | category | flops | bytes accessed | tf_op | source)
XLA Modules:
  0.0 21.4 jit_solution(12902512621461362072)
XLA Ops:
  0.0 20.7 %beam_power.1 = f32[32,256]{1,0:T(8,128)S(1)} custom-call(bf16[2,32,8,256]{3,2,1,0:T(8,128)(2,1)} %spectra.1, s32[2,2048]{1,0:T(2,128)} %coords_hbm.1, s32[2,2048]{1,0:T(2,128)} %slowness_hbm.1), custom_call_target="tpu_custom_call" | custom-call | tf_op jit(solution)/shard_map/beam_power/pallas_call | solution.py:387
  20.7 0.6 %copy.5 = f32[32,256]{1,0:T(8,128)} copy(f32[32,256]{1,0:T(8,128)S(1)} %beam_power.1) | data formatting | bytes 65536
where the time goes:
time: 21.5 us; the launch traced here: 21.4 us
  Pallas kernels  20.7 us (96%)
  local copies, waits for them, and re-layouts  0.62 us (3%)
    pallas_call x1, Pallas kernels, local(): pl.pallas_call(functools.partial(kernel, dims), out_shape=pltpu.VMEM((bin...  20.7 us
    unnamed x1, local copies, waits for them, and re-layouts  0.62 us

commit v1 on v0

--- a/solution.py
+++ b/solution.py
@@ -37,6 +37,7 @@
     coords,
     slowness,
     own,
+    white,
     blocks,
     squares,
     scales,
@@ -44,14 +45,15 @@
     sin_b,
     rotor,
     right,
+    turned,
     left,
     product,
     grid_hi_lo,
     onehot,
     picked,
     returned,
+    entered,
     own_sem,
-    local_sem,
     coords_sem,
     slow_sem,
     sq_send,
@@ -70,22 +72,51 @@
     lane_of = me % copies
     f32, bf16 = jnp.float32, jnp.bfloat16
 
-    def partner(o):
-        if n_sta & (n_sta - 1):
-            return (me + o) % n_sta
-        return me ^ o
-
-    def origin(o):
-        if n_sta & (n_sta - 1):
-            return (me - o + n_sta) % n_sta
-        return me ^ o
+    paired = n_sta >= 4 and n_sta & (n_sta - 1) == 0
+    half = n_sta // 2
+    upper = me // half if paired else 0
+
+    edge = n_sta // 4
+    raw = 2 if paired else 0
+
+    def partner(k):
+        if not paired:
+            return (me + k + 1) % n_sta
+        flip = me & 1
+        if k < 2:
+            early = half - 2 + k
+        elif k < half:
+            early = me ^ k ^ flip
+        elif k < n_sta - 2:
+            early = k - half
+        else:
+            early = me ^ 1 ^ flip
+        outer = n_sta - 2 if k == 0 else (n_sta - 1 if k == half - 1 else half + k - 1)
+        if k < half:
+            late = jnp.where(me < edge, outer, n_sta - 1 - k)
+        else:
+            late = me ^ (k - half + 2 if k < n_sta - 2 else 1) ^ flip
+        return jnp.where(upper == 1, early, late) ^ flip
+
+    def origin(k):
+        if not paired:
+            return (me - k - 1 + n_sta) % n_sta
+        inner = jnp.logical_and(me >= edge, me < half)
+        far = jnp.where(inner, k - 1, k - (half - 1))
+        aside = jnp.where(jnp.logical_and(inner, k > 0), k - half + 1, k + 1)
+        return jnp.where(
+            jnp.logical_and(far >= 0, far < half), (1 - upper) * half + far, me ^ aside
+        )
+
+    sends_raw = upper == 1
+
+    def is_raw(source):
+        return jnp.logical_and(
+            source // half == 1, jnp.logical_and(me >= half - 2, me < half)
+        )
 
     own_copy = pltpu.make_async_copy(spectra, own, own_sem)
     own_copy.start()
-    local_copy = pltpu.make_async_copy(
-        spectra.at[:, pl.ds(group * fb, fb)], blocks.at[me], local_sem
-    )
-    local_copy.start()
     coords_copy = pltpu.make_async_copy(coords_hbm, coords, coords_sem)
     coords_copy.start()
     slow_copy = pltpu.make_async_copy(slowness_hbm, slowness, slow_sem)
@@ -97,9 +128,13 @@
             barrier, inc=1, device_id={"bins": (mb + o) % n_bins}, device_id_type=MESH
         )
     for o in range(1, n_sta):
-        pl.semaphore_signal(
-            barrier, inc=1, device_id={"sta": partner(o)}, device_id_type=MESH
-        )
+        later = me + o
+
+        @pl.when(later < n_sta)
+        def _():
+            pl.semaphore_signal(
+                barrier, inc=1, device_id={"sta": later}, device_id_type=MESH
+            )
 
     own_copy.wait()
 
@@ -111,6 +146,97 @@
     squares[mb] = lax.fori_loop(
         0, bins_dev, square_step, jnp.zeros((segs, sta_dev), f32), unroll=True
     )
+
+    pl.semaphore_wait(barrier, n_bins - 1 + me)
+    for o in range(1, n_sta):
+        earlier = me - o
+
+        @pl.when(earlier >= 0)
+        def _():
+            pl.semaphore_signal(
+                entered.at[me], inc=1, device_id={"sta": earlier}, device_id_type=MESH
+            )
+
+
+    def square_send(o):
+        return pltpu.make_async_remote_copy(
+            src_ref=squares.at[mb],
+            dst_ref=squares.at[mb],
+            send_sem=sq_send.at[o],
+            recv_sem=sq_recv.at[mb],
+            device_id={"bins": (mb + o) % n_bins},
+            device_id_type=MESH,
+        )
+
+    def square_arrival(o):
+        source = (mb + o) % n_bins
+        return pltpu.make_async_remote_copy(
+            src_ref=squares.at[source],
+            dst_ref=squares.at[source],
+            send_sem=sq_send.at[o],
+            recv_sem=sq_recv.at[source],
+            device_id={"bins": source},
+            device_id_type=MESH,
+        )
+
+    def scale_send(k):
+        return pltpu.make_async_remote_copy(
+            src_ref=scales.at[me],
+            dst_ref=scales.at[me],
+            send_sem=sc_send.at[k],
+            recv_sem=sc_recv.at[me],
+            device_id={"sta": partner(k)},
+            device_id_type=MESH,
+        )
+
+    def scale_arrival(source):
+        return pltpu.make_async_remote_copy(
+            src_ref=scales.at[source],
+            dst_ref=scales.at[source],
+            send_sem=sc_send.at[0],
+            recv_sem=sc_recv.at[source],
+            device_id={"sta": source},
+            device_id_type=MESH,
+        )
+
+    def block_send(k, values):
+        target = partner(k)
+        return pltpu.make_async_remote_copy(
+            src_ref=values.at[:, pl.ds((target // copies) * fb, fb)],
+            dst_ref=blocks.at[me],
+            send_sem=bl_send.at[k],
+            recv_sem=bl_recv.at[me],
+            device_id={"sta": target},
+            device_id_type=MESH,
+        )
+
+    def await_entry(k):
+        target = partner(k)
+
+        @pl.when(target > me)
+        def _():
+            pl.semaphore_wait(entered.at[target], 1)
+
+    def block_arrival(source):
+        return pltpu.make_async_remote_copy(
+            src_ref=blocks.at[source],
+            dst_ref=blocks.at[source],
+            send_sem=bl_send.at[0],
+            recv_sem=bl_recv.at[source],
+            device_id={"sta": source},
+            device_id_type=MESH,
+        )
+
+    for o in range(1, n_bins):
+        square_send(o).start()
+    if raw:
+
+        @pl.when(sends_raw)
+        def _():
+            for k in range(raw):
+                await_entry(k)
+                block_send(k, own).start()
+
 
     coords_copy.wait()
     first_bin = mb * bins_dev + group * fb + 1
@@ -142,9 +268,40 @@
                 right[f, base + 160 : base + 176, at] = (sc - cs).astype(bf16)
         return carry
 
-    lax.fori_loop(0, fb * n_sta // 2, table_step, 0)
+    lax.fori_loop(0, fb * n_sta - fb * n_sta // 4, table_step, 0)
+
+    for o in range(1, n_bins):
+        square_arrival(o).wait_recv()
+    total = squares[0]
+    for b in range(1, n_bins):
+        total = total + squares[b]
+    inverse = 1.0 / jnp.sqrt(total / (2 * bins_dev * n_bins) + epsilon)
+    scales[me] = inverse
+    for f in range(bins_dev):
+        for c in range(2):
+            white[c, f] = (own[c, f].astype(f32) * inverse).astype(bf16)
+    if raw:
+
+        @pl.when(sends_raw)
+        def _():
+            for k in range(raw):
+                scale_send(k).start()
+
+        @pl.when(jnp.logical_not(sends_raw))
+        def _():
+            for k in range(raw):
+                await_entry(k)
+                block_send(k, white).start()
+
+    for k in range(raw, n_sta - 1):
+        await_entry(k)
+        block_send(k, white).start()
+    for f in range(fb):
+        for c in range(2):
+            blocks[me, c, f] = white[c, group * fb + f]
+
+    lax.fori_loop(fb * n_sta - fb * n_sta // 4, fb * n_sta, table_step, 0)
     product[...] = jnp.zeros_like(product)
-
     slow_copy.wait()
     sx = slowness[0:1, :] + 32
     sy = slowness[1:2, :] + 32
@@ -158,95 +315,20 @@
         ids = lax.broadcasted_iota(jnp.int32, (16, column.shape[1]), 0) + 16 * i
         onehot[i * 16 : (i + 1) * 16, :] = jnp.where(ids == column, 1.0, 0.0).astype(bf16)
 
-    pl.semaphore_wait(barrier, n_bins + n_sta - 2)
-
-    def square_send(o):
-        return pltpu.make_async_remote_copy(
-            src_ref=squares.at[mb],
-            dst_ref=squares.at[mb],
-            send_sem=sq_send.at[o],
-            recv_sem=sq_recv.at[mb],
-            device_id={"bins": (mb + o) % n_bins},
-            device_id_type=MESH,
-        )
-
-    def square_arrival(o):
-        source = (mb + o) % n_bins
-        return pltpu.make_async_remote_copy(
-            src_ref=squares.at[source],
-            dst_ref=squares.at[source],
-            send_sem=sq_send.at[o],
-            recv_sem=sq_recv.at[source],
-            device_id={"bins": source},
-            device_id_type=MESH,
-        )
-
-    def scale_send(o):
-        return pltpu.make_async_remote_copy(
-            src_ref=scales.at[me],
-            dst_ref=scales.at[me],
-            send_sem=sc_send.at[o],
-            recv_sem=sc_recv.at[me],
-            device_id={"sta": partner(o)},
-            device_id_type=MESH,
-        )
-
-    def scale_arrival(o):
-        source = origin(o)
-        return pltpu.make_async_remote_copy(
-            src_ref=scales.at[source],
-            dst_ref=scales.at[source],
-            send_sem=sc_send.at[o],
-            recv_sem=sc_recv.at[source],
-            device_id={"sta": source},
-            device_id_type=MESH,
-        )
-
-    def block_send(o):
-        target = partner(o)
-        return pltpu.make_async_remote_copy(
-            src_ref=own.at[:, pl.ds((target // copies) * fb, fb)],
-            dst_ref=blocks.at[me],
-            send_sem=bl_send.at[o],
-            recv_sem=bl_recv.at[me],
-            device_id={"sta": target},
-            device_id_type=MESH,
-        )
-
-    def block_arrival(o):
-        source = origin(o)
-        return pltpu.make_async_remote_copy(
-            src_ref=blocks.at[source],
-            dst_ref=blocks.at[source],
-            send_sem=bl_send.at[o],
-            recv_sem=bl_recv.at[source],
-            device_id={"sta": source},
-            device_id_type=MESH,
-        )
-
-    for o in range(1, n_bins):
-        square_send(o).start()
-    for o in range(n_sta - 1, 0, -1):
-        block_send(o).start()
-
-    lax.fori_loop(fb * n_sta // 2, fb * n_sta, table_step, 0)
-    for o in range(1, n_bins):
-        square_arrival(o).wait_recv()
-    total = squares[0]
-    for b in range(1, n_bins):
-        total = total + squares[b]
-    scales[me] = 1.0 / jnp.sqrt(total / (2 * bins_dev * n_bins) + epsilon)
-    for o in range(1, n_sta):
-        scale_send(o).start()
-
-    local_copy.wait()
-
-    def fill(o, source):
+
+    def turn_step(step, carry):
+        at = pl.ds(pl.multiple_of(step * sta_dev, sta_dev), sta_dev)
+        for f in range(fb):
+            turned[f, at, :] = right[f, :, at].T
+        return carry
+
+    lax.fori_loop(0, n_sta, turn_step, 0)
+
+    def fill(source):
         at = pl.ds(pl.multiple_of(source * sta_dev, sta_dev), sta_dev)
-        inverse = scales[source]
         for f in range(fb):
-            re = (blocks[source, 0, f].astype(f32) * inverse).astype(bf16).astype(f32)
-            im = (blocks[source, 1, f].astype(f32) * inverse).astype(bf16).astype(f32)
+            re = blocks[source, 0, f].astype(f32)
+            im = blocks[source, 1, f].astype(f32)
             c0 = rotor[f, 0, 2:3, at]
             s0 = rotor[f, 1, 2:3, at]
             parts = (re * c0 - im * s0, im * c0 + re * s0)
@@ -260,19 +342,30 @@
                         base = ((p * 2 + ri) * segs + g) * 8
                         left[f, base : base + 16, :] = both.astype(bf16)
             product[f] += lax.dot_general(
-                left[f], right[f, :, at], (((1,), (1,)), ((), ())), preferred_element_type=f32
+                left[f], turned[f, at, :], (((1,), (0,)), ((), ())), preferred_element_type=f32
             )
 
-    def arrive_step(o, carry):
-        @pl.when(o > 0)
-        def _():
-            block_arrival(o).wait_recv()
-            scale_arrival(o).wait_recv()
-
-        fill(o, origin(o))
+    def whiten(source):
+        scale_arrival(source).wait_recv()
+        factor = scales[source]
+        for f in range(fb):
+            for c in range(2):
+                blocks[source, c, f] = (blocks[source, c, f].astype(f32) * factor).astype(bf16)
+
+    def arrive_step(k, carry):
+        source = origin(k)
+        block_arrival(source).wait_recv()
+        if raw:
+
+            @pl.when(is_raw(source))
+            def _():
+                whiten(source)
+
+        fill(source)
         return carry
 
-    lax.fori_loop(0, n_sta, arrive_step, 0)
+    fill(me)
+    lax.fori_loop(0, n_sta - 1, arrive_step, 0)
 
     part = segs * 8
 
@@ -315,13 +408,13 @@
     )
 
     def result_send(o):
-        target = ((group + o) % groups) * copies + lane_of
-        return pltpu.make_async_remote_copy(
-            src_ref=picked.at[target],
+        there = (group + o) % groups
+        return pltpu.make_async_remote_copy(
+            src_ref=picked.at[there],
             dst_ref=returned.at[group],
             send_sem=re_send.at[o],
             recv_sem=re_recv.at[group],
-            device_id={"sta": target},
+            device_id={"sta": there * copies + lane_of},
             device_id_type=MESH,
         )
 
@@ -338,10 +431,12 @@
 
     ids16 = lax.broadcasted_iota(jnp.int32, (16, beams_dev), 0)
     packed_rows = 16 * fb
-    place = returned.at[group]
-    for o in list(range(1, groups)) + [0]:
-        target = ((group + o) % groups) * copies + lane_of
-        at = pl.ds(pl.multiple_of(target * beams_dev, beams_dev), beams_dev)
+    for there in range(groups):
+        if copies == 1:
+            at = pl.ds(there * beams_dev, beams_dev)
+        else:
+            target = there * copies + lane_of
+            at = pl.ds(pl.multiple_of(target * beams_dev, beams_dev), beams_dev)
         values = jnp.dot(rows, onehot[:, at], preferred_element_type=f32)
         values = values[:packed_rows] + values[packed_rows:]
         sx_at = slowness[0:1, at] + 32
@@ -350,12 +445,10 @@
         keep = jnp.where(ids16 == row_at, norm, 0.0)
         for f in range(fb):
             line = jnp.sum(values[f * 16 : (f + 1) * 16] * keep, axis=0, keepdims=True)
-            if o:
-                picked[target, f : f + 1, :] = line
-            else:
-                place[f : f + 1, :] = line
-        if o:
-            result_send(o).start()
+            picked[there, f : f + 1, :] = line
+    for o in range(1, groups):
+        result_send(o).start()
+    returned[group] = picked[group]
 
     for o in range(1, groups):
         result_arrival(o).wait_recv()
@@ -364,9 +457,15 @@
 
     for o in range(1, n_bins):
         square_send(o).wait_send()
-    for o in range(1, n_sta):
-        block_send(o).wait_send()
-        scale_send(o).wait_send()
+    for k in range(n_sta - 1):
+        block_send(k, white).wait_send()
+    if raw:
+
+        @pl.when(sends_raw)
+        def _():
+            for k in range(raw):
+                scale_send(k).wait_send()
+
     for o in range(1, groups):
         result_send(o).wait_send()
 
@@ -397,6 +496,7 @@
                 pltpu.VMEM((2, stations), jnp.int32),
                 pltpu.VMEM((2, beams), jnp.int32),
                 pltpu.VMEM((2, bins_dev, segs, sta_dev), bf16),
+                pltpu.VMEM((2, bins_dev, segs, sta_dev), bf16),
                 pltpu.VMEM((n_sta, 2, fb, segs, sta_dev), bf16),
                 pltpu.VMEM((n_bins, segs, sta_dev), f32),
                 pltpu.VMEM((n_sta, segs, sta_dev), f32),
@@ -404,19 +504,20 @@
                 pltpu.VMEM((fb, 8, stations), f32),
                 pltpu.VMEM((fb, 2, 8, stations), f32),
                 pltpu.VMEM((fb, 256, stations), bf16),
+                pltpu.VMEM((fb, stations, 256), bf16),
                 pltpu.VMEM((fb, 32 * segs, sta_dev), bf16),
                 pltpu.VMEM((fb, 32 * segs, 256), f32),
                 pltpu.VMEM((2, fb, 16, 256), bf16),
                 pltpu.VMEM((256, beams), bf16),
                 pltpu.VMEM((n_sta, fb, beams_dev), f32),
                 pltpu.VMEM((groups, fb, beams_dev), f32),
-                dma,
+                pltpu.SemaphoreType.REGULAR((n_sta,)),
                 dma,
                 dma,
                 dma,
                 dma((n_bins,)),
                 dma((n_bins,)),
-                dma((n_sta,)),
+                dma((max(2, n_sta),)),
                 dma((n_sta,)),
                 dma((n_sta,)),
                 dma((n_sta,)),

time: 21.5 us -> 20.4 us (0.949)
  Pallas kernels: 20.7 us -> 19.6 us
    pallas_call x1, Pallas kernels: 20.7 us -> 19.6 us  [local(): pl.pallas_call(functools.partial(kernel, dims), out_shape=pltpu.VMEM((bin...]
where the time goes in v1:
time: 20.4 us; the launch traced here: 20.2 us
  Pallas kernels  19.6 us (96%)
  local copies, waits for them, and re-layouts  0.62 us (3%)
    pallas_call x1, Pallas kernels, local(): pl.pallas_call(functools.partial(kernel, dims), out_shape=pltpu.VMEM((bin...  19.6 us
    unnamed x1, local copies, waits for them, and re-layouts  0.62 us

profile of v1, /device:TPU:0, one launch (start us, length us, event | category | flops | bytes accessed | tf_op | source)
XLA Modules:
  0.0 20.2 jit_solution(692215727219185843)
XLA Ops:
  0.0 19.6 %beam_power.1 = f32[32,256]{1,0:T(8,128)S(1)} custom-call(bf16[2,32,8,256]{3,2,1,0:T(8,128)(2,1)} %spectra.1, s32[2,2048]{1,0:T(2,128)} %coords_hbm.1, s32[2,2048]{1,0:T(2,128)} %slowness_hbm.1), custom_call_target="tpu_custom_call" | custom-call | tf_op jit(solution)/shard_map/beam_power/pallas_call | solution.py:486
  19.6 0.6 %copy.5 = f32[32,256]{1,0:T(8,128)} copy(f32[32,256]{1,0:T(8,128)S(1)} %beam_power.1) | data formatting | bytes 65536

commit v2 on v1

--- a/solution.py
+++ b/solution.py
@@ -50,6 +50,7 @@
     product,
     grid_hi_lo,
     onehot,
+    keep,
     picked,
     returned,
     entered,
@@ -65,12 +66,13 @@
     re_send,
     re_recv,
 ):
-    n_bins, n_sta, groups, copies, fb, bins_dev, segs, sta_dev, beams_dev = dims
+    n_bins, n_sta, groups, copies, fb, extra, bins_dev, segs, sta_dev, beams_dev = dims
     me = lax.axis_index("sta")
     mb = lax.axis_index("bins")
     group = me // copies
     lane_of = me % copies
     f32, bf16 = jnp.float32, jnp.bfloat16
+    most = fb + extra
 
     paired = n_sta >= 4 and n_sta & (n_sta - 1) == 0
     half = n_sta // 2
@@ -91,9 +93,8 @@
             early = k - half
         else:
             early = me ^ 1 ^ flip
-        outer = n_sta - 2 if k == 0 else (n_sta - 1 if k == half - 1 else half + k - 1)
         if k < half:
-            late = jnp.where(me < edge, outer, n_sta - 1 - k)
+            late = half + k if half < 4 else ((half, n_sta - 2, n_sta - 1)[k] if k < 3 else half + k - 2)
         else:
             late = me ^ (k - half + 2 if k < n_sta - 2 else 1) ^ flip
         return jnp.where(upper == 1, early, late) ^ flip
@@ -104,11 +105,22 @@
         inner = jnp.logical_and(me >= edge, me < half)
         far = jnp.where(inner, k - 1, k - (half - 1))
         aside = jnp.where(jnp.logical_and(inner, k > 0), k - half + 1, k + 1)
-        return jnp.where(
-            jnp.logical_and(far >= 0, far < half), (1 - upper) * half + far, me ^ aside
-        )
-
+        other = jnp.where(upper == 1, far, jnp.where(me < edge, n_sta - 1 - far, half + far))
+        return jnp.where(jnp.logical_and(far >= 0, far < half), other, me ^ aside)
+
+    def first_of(part):
+        if extra:
+            return part * most - jnp.maximum(part - half, 0) * extra
+        return part * fb
+
+    def is_long(part):
+        return part < half
+
+    long_me = is_long(group)
+    bins_me = jnp.where(long_me, most, fb)
+    first_me = first_of(group)
     sends_raw = upper == 1
+    prompt = mb % 2 == 0
 
     def is_raw(source):
         return jnp.logical_and(
@@ -162,20 +174,19 @@
         return pltpu.make_async_remote_copy(
             src_ref=squares.at[mb],
             dst_ref=squares.at[mb],
-            send_sem=sq_send.at[o],
-            recv_sem=sq_recv.at[mb],
+            send_sem=sq_send,
+            recv_sem=sq_recv,
             device_id={"bins": (mb + o) % n_bins},
             device_id_type=MESH,
         )
 
-    def square_arrival(o):
-        source = (mb + o) % n_bins
-        return pltpu.make_async_remote_copy(
-            src_ref=squares.at[source],
-            dst_ref=squares.at[source],
-            send_sem=sq_send.at[o],
-            recv_sem=sq_recv.at[source],
-            device_id={"bins": source},
+    def squares_of(count):
+        return pltpu.make_async_remote_copy(
+            src_ref=squares.at[pl.ds(0, count)],
+            dst_ref=squares.at[pl.ds(0, count)],
+            send_sem=sq_send,
+            recv_sem=sq_recv,
+            device_id={"bins": mb},
             device_id_type=MESH,
         )
 
@@ -183,8 +194,8 @@
         return pltpu.make_async_remote_copy(
             src_ref=scales.at[me],
             dst_ref=scales.at[me],
-            send_sem=sc_send.at[k],
-            recv_sem=sc_recv.at[me],
+            send_sem=sc_send,
+            recv_sem=sc_recv.at[me - half],
             device_id={"sta": partner(k)},
             device_id_type=MESH,
         )
@@ -193,23 +204,64 @@
         return pltpu.make_async_remote_copy(
             src_ref=scales.at[source],
             dst_ref=scales.at[source],
-            send_sem=sc_send.at[0],
-            recv_sem=sc_recv.at[source],
+            send_sem=sc_send,
+            recv_sem=sc_recv.at[source - half],
             device_id={"sta": source},
             device_id_type=MESH,
         )
 
-    def block_send(k, values):
+    def block_copy(k, values, begin, count):
         target = partner(k)
         return pltpu.make_async_remote_copy(
-            src_ref=values.at[:, pl.ds((target // copies) * fb, fb)],
-            dst_ref=blocks.at[me],
-            send_sem=bl_send.at[k],
+            src_ref=values.at[:, pl.ds(first_of(target // copies) + begin, count)],
+            dst_ref=blocks.at[me, :, pl.ds(begin, count)],
+            send_sem=bl_send,
             recv_sem=bl_recv.at[me],
             device_id={"sta": target},
             device_id_type=MESH,
         )
 
+    def block_send(k, values):
+        block_copy(k, values, 0, fb).start()
+        if extra:
+
+            @pl.when(is_long(partner(k)))
+            def _():
+                block_copy(k, values, fb, extra).start()
+
+    def blocks_sent():
+        def wait(ref):
+            pltpu.make_async_remote_copy(
+                src_ref=ref,
+                dst_ref=ref,
+                send_sem=bl_send,
+                recv_sem=bl_recv.at[me],
+                device_id={"sta": me},
+                device_id_type=MESH,
+            ).wait_send()
+
+        if not extra:
+            wait(blocks.at[pl.ds(0, n_sta - 1)])
+            return
+
+        @pl.when(long_me)
+        def _():
+            wait(white.at[:, pl.ds(0, bins_dev - most)])
+
+        @pl.when(jnp.logical_not(long_me))
+        def _():
+            wait(white.at[:, pl.ds(0, bins_dev - fb)])
+
+    def scales_of(count):
+        return pltpu.make_async_remote_copy(
+            src_ref=scales.at[pl.ds(0, count)],
+            dst_ref=scales.at[pl.ds(0, count)],
+            send_sem=sc_send,
+            recv_sem=sc_recv.at[0],
+            device_id={"sta": me},
+            device_id_type=MESH,
+        )
+
     def await_entry(k):
         target = partner(k)
 
@@ -217,11 +269,11 @@
         def _():
             pl.semaphore_wait(entered.at[target], 1)
 
-    def block_arrival(source):
-        return pltpu.make_async_remote_copy(
-            src_ref=blocks.at[source],
-            dst_ref=blocks.at[source],
-            send_sem=bl_send.at[0],
+    def block_arrival(source, count):
+        return pltpu.make_async_remote_copy(
+            src_ref=blocks.at[source, :, pl.ds(0, count)],
+            dst_ref=blocks.at[source, :, pl.ds(0, count)],
+            send_sem=bl_send,
             recv_sem=bl_recv.at[source],
             device_id={"sta": source},
             device_id_type=MESH,
@@ -235,11 +287,11 @@
         def _():
             for k in range(raw):
                 await_entry(k)
-                block_send(k, own).start()
+                block_send(k, own)
 
 
     coords_copy.wait()
-    first_bin = mb * bins_dev + group * fb + 1
+    first_bin = mb * bins_dev + first_me + 1
 
     def table_step(step, carry):
         f = step // n_sta
@@ -268,10 +320,10 @@
                 right[f, base + 160 : base + 176, at] = (sc - cs).astype(bf16)
         return carry
 
-    lax.fori_loop(0, fb * n_sta - fb * n_sta // 4, table_step, 0)
-
-    for o in range(1, n_bins):
-        square_arrival(o).wait_recv()
+    lax.fori_loop(0, fb * n_sta, table_step, 0)
+
+    if n_bins > 1:
+        squares_of(n_bins - 1).wait_recv()
     total = squares[0]
     for b in range(1, n_bins):
         total = total + squares[b]
@@ -287,20 +339,39 @@
             for k in range(raw):
                 scale_send(k).start()
 
-        @pl.when(jnp.logical_not(sends_raw))
-        def _():
-            for k in range(raw):
-                await_entry(k)
-                block_send(k, white).start()
-
-    for k in range(raw, n_sta - 1):
-        await_entry(k)
-        block_send(k, white).start()
+    def crosses(k):
+        late_far = 1 if k < half else 0
+        early_far = 1 if half <= k < n_sta - 2 else 0
+        return jnp.where(upper == 1, early_far, late_far) == 1
+
+    def white_send(k, wanted):
+        if k < raw:
+            wanted = jnp.logical_and(wanted, jnp.logical_not(sends_raw))
+
+        @pl.when(wanted)
+        def _():
+            await_entry(k)
+            block_send(k, white)
+
+    for k in range(n_sta - 1):
+        if paired:
+            white_send(k, jnp.logical_or(prompt, jnp.logical_not(crosses(k))))
+        else:
+            white_send(k, True)
+
     for f in range(fb):
         for c in range(2):
-            blocks[me, c, f] = white[c, group * fb + f]
-
-    lax.fori_loop(fb * n_sta - fb * n_sta // 4, fb * n_sta, table_step, 0)
+            blocks[me, c, f] = white[c, first_me + f]
+    if extra:
+
+        @pl.when(long_me)
+        def _():
+            for f in range(fb, most):
+                for c in range(2):
+                    blocks[me, c, f] = white[c, first_me + f]
+
+    if extra:
+        lax.fori_loop(fb * n_sta, bins_me * n_sta, table_step, 0)
     product[...] = jnp.zeros_like(product)
     slow_copy.wait()
     sx = slowness[0:1, :] + 32
@@ -314,19 +385,40 @@
     for i in range(16):
         ids = lax.broadcasted_iota(jnp.int32, (16, column.shape[1]), 0) + 16 * i
         onehot[i * 16 : (i + 1) * 16, :] = jnp.where(ids == column, 1.0, 0.0).astype(bf16)
-
-
-    def turn_step(step, carry):
-        at = pl.ds(pl.multiple_of(step * sta_dev, sta_dev), sta_dev)
-        for f in range(fb):
-            turned[f, at, :] = right[f, :, at].T
-        return carry
-
-    lax.fori_loop(0, n_sta, turn_step, 0)
-
-    def fill(source):
+    norm = 1.0 / (n_sta * sta_dev * segs)
+    b_index = sx % 16
+    row = jnp.where(b_index >= 8, b_index - 8, 15 - b_index)
+    ids = lax.broadcasted_iota(jnp.int32, (16, column.shape[1]), 0)
+    keep[...] = jnp.where(ids == row, norm, 0.0)
+
+
+    def turn(begin, end):
+        def turn_step(step, carry):
+            at = pl.ds(pl.multiple_of(step * sta_dev, sta_dev), sta_dev)
+            for f in range(begin, end):
+                turned[f, at, :] = right[f, :, at].T
+            return carry
+
+        lax.fori_loop(0, n_sta, turn_step, 0)
+
+    def late_sends(when):
+        for k in range(n_sta - 2):
+            white_send(k, jnp.logical_and(jnp.logical_and(jnp.logical_not(prompt), when), crosses(k)))
+
+    if paired:
+        late_sends(upper == 0)
+    turn(0, fb)
+    if paired:
+        late_sends(upper == 1)
+    if extra:
+
+        @pl.when(long_me)
+        def _():
+            turn(fb, most)
+
+    def fill(source, count):
         at = pl.ds(pl.multiple_of(source * sta_dev, sta_dev), sta_dev)
-        for f in range(fb):
+        for f in range(count):
             re = blocks[source, 0, f].astype(f32)
             im = blocks[source, 1, f].astype(f32)
             c0 = rotor[f, 0, 2:3, at]
@@ -345,27 +437,44 @@
                 left[f], turned[f, at, :], (((1,), (0,)), ((), ())), preferred_element_type=f32
             )
 
-    def whiten(source):
+    def whiten(source, count):
         scale_arrival(source).wait_recv()
         factor = scales[source]
-        for f in range(fb):
+        for f in range(count):
             for c in range(2):
                 blocks[source, c, f] = (blocks[source, c, f].astype(f32) * factor).astype(bf16)
 
+    def take(k, count, may_be_raw):
+        source = jnp.where(k == 0, me, origin(k - 1))
+
+        @pl.when(k > 0)
+        def _():
+            block_arrival(source, count).wait_recv()
+
+        if may_be_raw:
+
+            @pl.when(jnp.logical_and(k > 0, is_raw(source)))
+            def _():
+                whiten(source, count)
+
+        fill(source, count)
+
     def arrive_step(k, carry):
-        source = origin(k)
-        block_arrival(source).wait_recv()
-        if raw:
-
-            @pl.when(is_raw(source))
-            def _():
-                whiten(source)
-
-        fill(source)
+        if not extra:
+            take(k, fb, raw > 0)
+            return carry
+
+        @pl.when(long_me)
+        def _():
+            take(k, most, True)
+
+        @pl.when(jnp.logical_not(long_me))
+        def _():
+            take(k, fb, False)
+
         return carry
 
-    fill(me)
-    lax.fori_loop(0, n_sta - 1, arrive_step, 0)
+    lax.fori_loop(0, n_sta, arrive_step, 0)
 
     part = segs * 8
 
@@ -400,38 +509,34 @@
         grid_hi_lo[1, f] = lo
         return carry
 
-    lax.fori_loop(0, fb, bin_power, 0)
-
-    norm = 1.0 / (n_sta * sta_dev * segs)
+    lax.fori_loop(0, most, bin_power, 0)
+
     rows = jnp.concatenate(
-        [grid_hi_lo[h, f] for h in range(2) for f in range(fb)], 0
+        [grid_hi_lo[h, f] for h in range(2) for f in range(most)], 0
     )
 
-    def result_send(o):
-        there = (group + o) % groups
+    def result_send(there):
         return pltpu.make_async_remote_copy(
             src_ref=picked.at[there],
             dst_ref=returned.at[group],
-            send_sem=re_send.at[o],
-            recv_sem=re_recv.at[group],
+            send_sem=re_send,
+            recv_sem=re_recv,
             device_id={"sta": there * copies + lane_of},
             device_id_type=MESH,
         )
 
-    def result_arrival(o):
-        source = (group + o) % groups
-        return pltpu.make_async_remote_copy(
-            src_ref=returned.at[source],
-            dst_ref=returned.at[source],
-            send_sem=re_send.at[o],
-            recv_sem=re_recv.at[source],
-            device_id={"sta": source * copies + lane_of},
-            device_id_type=MESH,
-        )
-
-    ids16 = lax.broadcasted_iota(jnp.int32, (16, beams_dev), 0)
-    packed_rows = 16 * fb
-    for there in range(groups):
+    def results_of(count):
+        return pltpu.make_async_remote_copy(
+            src_ref=returned.at[pl.ds(0, count)],
+            dst_ref=returned.at[pl.ds(0, count)],
+            send_sem=re_send,
+            recv_sem=re_recv,
+            device_id={"sta": me},
+            device_id_type=MESH,
+        )
+
+    packed_rows = 16 * most
+    def pick(there):
         if copies == 1:
             at = pl.ds(there * beams_dev, beams_dev)
         else:
@@ -439,35 +544,41 @@
             at = pl.ds(pl.multiple_of(target * beams_dev, beams_dev), beams_dev)
         values = jnp.dot(rows, onehot[:, at], preferred_element_type=f32)
         values = values[:packed_rows] + values[packed_rows:]
-        sx_at = slowness[0:1, at] + 32
-        b_at = sx_at % 16
-        row_at = jnp.where(b_at >= 8, b_at - 8, 15 - b_at)
-        keep = jnp.where(ids16 == row_at, norm, 0.0)
-        for f in range(fb):
-            line = jnp.sum(values[f * 16 : (f + 1) * 16] * keep, axis=0, keepdims=True)
+        for f in range(most):
+            line = jnp.sum(values[f * 16 : (f + 1) * 16] * keep[:, at], axis=0, keepdims=True)
             picked[there, f : f + 1, :] = line
-    for o in range(1, groups):
-        result_send(o).start()
+
+    soon = min(2, groups)
+    for span in (range(soon), range(soon, groups)):
+        for there in span:
+            pick(there)
+        for there in span:
+
+            @pl.when(there != group)
+            def _():
+                result_send(there).start()
+
     returned[group] = picked[group]
 
-    for o in range(1, groups):
-        result_arrival(o).wait_recv()
+    if groups > 1:
+        results_of(groups - 1).wait_recv()
     for g in range(groups):
-        out[g * fb : (g + 1) * fb, :] = returned[g]
-
-    for o in range(1, n_bins):
-        square_send(o).wait_send()
-    for k in range(n_sta - 1):
-        block_send(k, white).wait_send()
+        count = most if not extra or g < half else fb
+        begin = g * most - max(g - half, 0) * extra
+        out[begin : begin + count, :] = returned[g, :count]
+
+    if n_bins > 1:
+        squares_of(n_bins - 1).wait_send()
+    if n_sta > 1:
+        blocks_sent()
     if raw:
 
         @pl.when(sends_raw)
         def _():
-            for k in range(raw):
-                scale_send(k).wait_send()
-
-    for o in range(1, groups):
-        result_send(o).wait_send()
+            scales_of(raw).wait_send()
+
+    if groups > 1:
+        results_of(groups - 1).wait_send()
 
 
 def solution(mesh):
@@ -480,7 +591,12 @@
         groups = math.gcd(bins_dev, n_sta)
         copies = n_sta // groups
         fb = bins_dev // groups
-        dims = (n_bins, n_sta, groups, copies, fb, bins_dev, segs, sta_dev, beams_dev)
+        extra = 0
+        if copies == 1 and n_sta >= 4 and n_sta & (n_sta - 1) == 0 and fb >= 4:
+            extra = 2 * (fb // 4)
+            fb = fb - fb // 4
+        most = fb + extra
+        dims = (n_bins, n_sta, groups, copies, fb, extra, bins_dev, segs, sta_dev, beams_dev)
         f32, bf16 = jnp.float32, jnp.bfloat16
         dma = pltpu.SemaphoreType.DMA
         return pl.pallas_call(
@@ -497,32 +613,33 @@
                 pltpu.VMEM((2, beams), jnp.int32),
                 pltpu.VMEM((2, bins_dev, segs, sta_dev), bf16),
                 pltpu.VMEM((2, bins_dev, segs, sta_dev), bf16),
-                pltpu.VMEM((n_sta, 2, fb, segs, sta_dev), bf16),
+                pltpu.VMEM((n_sta, 2, most, segs, sta_dev), bf16),
                 pltpu.VMEM((n_bins, segs, sta_dev), f32),
                 pltpu.VMEM((n_sta, segs, sta_dev), f32),
-                pltpu.VMEM((fb, 8, stations), f32),
-                pltpu.VMEM((fb, 8, stations), f32),
-                pltpu.VMEM((fb, 2, 8, stations), f32),
-                pltpu.VMEM((fb, 256, stations), bf16),
-                pltpu.VMEM((fb, stations, 256), bf16),
-                pltpu.VMEM((fb, 32 * segs, sta_dev), bf16),
-                pltpu.VMEM((fb, 32 * segs, 256), f32),
-                pltpu.VMEM((2, fb, 16, 256), bf16),
+                pltpu.VMEM((most, 8, stations), f32),
+                pltpu.VMEM((most, 8, stations), f32),
+                pltpu.VMEM((most, 2, 8, stations), f32),
+                pltpu.VMEM((most, 256, stations), bf16),
+                pltpu.VMEM((most, stations, 256), bf16),
+                pltpu.VMEM((most, 32 * segs, sta_dev), bf16),
+                pltpu.VMEM((most, 32 * segs, 256), f32),
+                pltpu.VMEM((2, most, 16, 256), bf16),
                 pltpu.VMEM((256, beams), bf16),
-                pltpu.VMEM((n_sta, fb, beams_dev), f32),
-                pltpu.VMEM((groups, fb, beams_dev), f32),
+                pltpu.VMEM((16, beams), f32),
+                pltpu.VMEM((n_sta, most, beams_dev), f32),
+                pltpu.VMEM((groups, most, beams_dev), f32),
                 pltpu.SemaphoreType.REGULAR((n_sta,)),
                 dma,
                 dma,
                 dma,
-                dma((n_bins,)),
-                dma((n_bins,)),
-                dma((max(2, n_sta),)),
+                dma,
+                dma,
+                dma,
+                dma((max(1, n_sta // 2),)),
+                dma,
                 dma((n_sta,)),
-                dma((n_sta,)),
-                dma((n_sta,)),
-                dma((groups,)),
-                dma((groups,)),
+                dma,
+                dma,
             ],
             compiler_params=pltpu.CompilerParams(
                 collective_id=0,

time: 20.4 us -> 19.3 us (0.946)
  Pallas kernels: 19.6 us -> 18.5 us
    pallas_call x1, Pallas kernels: 19.6 us -> 18.5 us  [local(): pl.pallas_call(functools.partial(kernel, dims), out_shape=pltpu.VMEM((bin...]
where the time goes in v2:
time: 19.3 us; the launch traced here: 19.2 us
  Pallas kernels  18.5 us (96%)
  local copies, waits for them, and re-layouts  0.62 us (3%)
    pallas_call x1, Pallas kernels, local(): pl.pallas_call(functools.partial(kernel, dims), out_shape=pltpu.VMEM((bin...  18.5 us
    unnamed x1, local copies, waits for them, and re-layouts  0.62 us

profile of v2, /device:TPU:0, one launch (start us, length us, event | category | flops | bytes accessed | tf_op | source)
XLA Modules:
  0.0 19.2 jit_solution(13239077898161255342)
XLA Ops:
  0.0 18.5 %beam_power.1 = f32[32,256]{1,0:T(8,128)S(1)} custom-call(bf16[2,32,8,256]{3,2,1,0:T(8,128)(2,1)} %spectra.1, s32[2,2048]{1,0:T(2,128)} %coords_hbm.1, s32[2,2048]{1,0:T(2,128)} %slowness_hbm.1), custom_call_target="tpu_custom_call" | custom-call | tf_op jit(solution)/shard_map/beam_power/pallas_call | solution.py:602
  18.5 0.6 %copy.5 = f32[32,256]{1,0:T(8,128)} copy(f32[32,256]{1,0:T(8,128)S(1)} %beam_power.1) | data formatting | bytes 65536

commit v3 on v2

--- a/solution.py
+++ b/solution.py
@@ -95,6 +95,12 @@
             early = me ^ 1 ^ flip
         if k < half:
             late = half + k if half < 4 else ((half, n_sta - 2, n_sta - 1)[k] if k < 3 else half + k - 2)
+            across = me + edge
+            rest = n_sta - k
+            rest = across if k == 0 else rest - jnp.where(rest <= across, 1, 0)
+            if k in (1, 2) and half >= 4:
+                rest = rest ^ (1 - flip)
+            late = jnp.where(me < edge, late, rest ^ flip)
         else:
             late = me ^ (k - half + 2 if k < n_sta - 2 else 1) ^ flip
         return jnp.where(upper == 1, early, late) ^ flip
@@ -102,11 +108,21 @@
     def origin(k):
         if not paired:
             return (me - k - 1 + n_sta) % n_sta
-        inner = jnp.logical_and(me >= edge, me < half)
-        far = jnp.where(inner, k - 1, k - (half - 1))
-        aside = jnp.where(jnp.logical_and(inner, k > 0), k - half + 1, k + 1)
-        other = jnp.where(upper == 1, far, jnp.where(me < edge, n_sta - 1 - far, half + far))
-        return jnp.where(jnp.logical_and(far >= 0, far < half), other, me ^ aside)
+        outer = k - (half - 1)
+        spread = half + outer
+        if half >= 4:
+            spread = jnp.where(outer == 0, half, n_sta - 3 + outer)
+            spread = jnp.where(outer > 2, half + outer - 2, spread)
+        at_edge = jnp.where(outer < 0, me ^ (k + 1), spread ^ (me & 1))
+        at_inner = jnp.where(k < half, half + k, me ^ (k - half + 1))
+        side = me & 1
+        at_upper = jnp.where(k == 0, me ^ 1, k - 1)
+        if half >= 4:
+            cross = 2 * (n_sta - 2 - k) + 1 - side
+            at_upper = jnp.where(k < half + half // 2 - 1, me ^ (k - half // 2 + 1), cross)
+            at_upper = jnp.where(k < half // 2 + 2, 2 * (k - 2) + side, at_upper)
+            at_upper = jnp.where(k < 2, me ^ (k + 1), at_upper)
+        return jnp.where(upper == 1, at_upper, jnp.where(me < edge, at_edge, at_inner))
 
     def first_of(part):
         if extra:
@@ -119,13 +135,26 @@
     long_me = is_long(group)
     bins_me = jnp.where(long_me, most, fb)
     first_me = first_of(group)
-    sends_raw = upper == 1
     prompt = mb % 2 == 0
 
+    inner = jnp.logical_and(me >= edge, me < half)
+
+    def sent_raw(k):
+        if not raw or k >= raw:
+            return False
+        return jnp.logical_or(upper == 1, inner) if k == 0 else upper == 1
+
     def is_raw(source):
-        return jnp.logical_and(
+        from_far = jnp.logical_and(
             source // half == 1, jnp.logical_and(me >= half - 2, me < half)
         )
+        from_near = jnp.logical_and(
+            source == me - edge, jnp.logical_and(me >= half, me < half + edge)
+        )
+        return jnp.logical_or(from_far, from_near)
+
+    def scale_slot(source):
+        return jnp.maximum(source - half, 0)
 
     own_copy = pltpu.make_async_copy(spectra, own, own_sem)
     own_copy.start()
@@ -195,7 +224,7 @@
             src_ref=scales.at[me],
             dst_ref=scales.at[me],
             send_sem=sc_send,
-            recv_sem=sc_recv.at[me - half],
+            recv_sem=sc_recv.at[scale_slot(me)],
             device_id={"sta": partner(k)},
             device_id_type=MESH,
         )
@@ -205,7 +234,7 @@
             src_ref=scales.at[source],
             dst_ref=scales.at[source],
             send_sem=sc_send,
-            recv_sem=sc_recv.at[source - half],
+            recv_sem=sc_recv.at[scale_slot(source)],
             device_id={"sta": source},
             device_id_type=MESH,
         )
@@ -281,14 +310,15 @@
 
     for o in range(1, n_bins):
         square_send(o).start()
-    if raw:
-
-        @pl.when(sends_raw)
-        def _():
-            for k in range(raw):
+    def raw_sends(when):
+        for k in range(raw):
+
+            @pl.when(jnp.logical_and(sent_raw(k), when))
+            def _():
                 await_entry(k)
                 block_send(k, own)
 
+    raw_sends(upper == 1)
 
     coords_copy.wait()
     first_bin = mb * bins_dev + first_me + 1
@@ -320,7 +350,10 @@
                 right[f, base + 160 : base + 176, at] = (sc - cs).astype(bf16)
         return carry
 
-    lax.fori_loop(0, fb * n_sta, table_step, 0)
+    most_steps = fb * n_sta - fb * n_sta // 4
+    lax.fori_loop(0, most_steps, table_step, 0)
+    raw_sends(inner)
+    lax.fori_loop(most_steps, fb * n_sta, table_step, 0)
 
     if n_bins > 1:
         squares_of(n_bins - 1).wait_recv()
@@ -332,12 +365,11 @@
     for f in range(bins_dev):
         for c in range(2):
             white[c, f] = (own[c, f].astype(f32) * inverse).astype(bf16)
-    if raw:
-
-        @pl.when(sends_raw)
-        def _():
-            for k in range(raw):
-                scale_send(k).start()
+    for k in range(raw):
+
+        @pl.when(sent_raw(k))
+        def _():
+            scale_send(k).start()
 
     def crosses(k):
         late_far = 1 if k < half else 0
@@ -346,7 +378,7 @@
 
     def white_send(k, wanted):
         if k < raw:
-            wanted = jnp.logical_and(wanted, jnp.logical_not(sends_raw))
+            wanted = jnp.logical_and(wanted, jnp.logical_not(sent_raw(k)))
 
         @pl.when(wanted)
         def _():
@@ -470,7 +502,7 @@
 
         @pl.when(jnp.logical_not(long_me))
         def _():
-            take(k, fb, False)
+            take(k, fb, True)
 
         return carry
 
@@ -509,7 +541,7 @@
         grid_hi_lo[1, f] = lo
         return carry
 
-    lax.fori_loop(0, most, bin_power, 0)
+    lax.fori_loop(0, bins_me if extra else most, bin_power, 0)
 
     rows = jnp.concatenate(
         [grid_hi_lo[h, f] for h in range(2) for f in range(most)], 0
@@ -571,11 +603,11 @@
         squares_of(n_bins - 1).wait_send()
     if n_sta > 1:
         blocks_sent()
-    if raw:
-
-        @pl.when(sends_raw)
-        def _():
-            scales_of(raw).wait_send()
+    for k in range(raw):
+
+        @pl.when(sent_raw(k))
+        def _():
+            scales_of(1).wait_send()
 
     if groups > 1:
         results_of(groups - 1).wait_send()

time: 19.3 us -> 19 us (0.984)
  Pallas kernels: 18.5 us -> 18.3 us
    pallas_call x1, Pallas kernels: 18.5 us -> 18.3 us  [local(): pl.pallas_call(functools.partial(kernel, dims), out_shape=pltpu.VMEM((bin...]
where the time goes in v3:
time: 19 us; the launch traced here: 18.9 us
  Pallas kernels  18.3 us (96%)
  local copies, waits for them, and re-layouts  0.62 us (3%)
    pallas_call x1, Pallas kernels, local(): pl.pallas_call(functools.partial(kernel, dims), out_shape=pltpu.VMEM((bin...  18.3 us
    unnamed x1, local copies, waits for them, and re-layouts  0.62 us

profile of v3, /device:TPU:0, one launch (start us, length us, event | category | flops | bytes accessed | tf_op | source)
XLA Modules:
  0.0 18.9 jit_solution(11492741920659921030)
XLA Ops:
  0.0 18.3 %beam_power.1 = f32[32,256]{1,0:T(8,128)S(1)} custom-call(bf16[2,32,8,256]{3,2,1,0:T(8,128)(2,1)} %spectra.1, s32[2,2048]{1,0:T(2,128)} %coords_hbm.1, s32[2,2048]{1,0:T(2,128)} %slowness_hbm.1), custom_call_target="tpu_custom_call" | custom-call | tf_op jit(solution)/shard_map/beam_power/pallas_call | solution.py:634
  18.3 0.6 %copy.5 = f32[32,256]{1,0:T(8,128)} copy(f32[32,256]{1,0:T(8,128)S(1)} %beam_power.1) | data formatting | bytes 65536

commit v4 on v3

--- a/solution.py
+++ b/solution.py
@@ -355,55 +355,6 @@
     raw_sends(inner)
     lax.fori_loop(most_steps, fb * n_sta, table_step, 0)
 
-    if n_bins > 1:
-        squares_of(n_bins - 1).wait_recv()
-    total = squares[0]
-    for b in range(1, n_bins):
-        total = total + squares[b]
-    inverse = 1.0 / jnp.sqrt(total / (2 * bins_dev * n_bins) + epsilon)
-    scales[me] = inverse
-    for f in range(bins_dev):
-        for c in range(2):
-            white[c, f] = (own[c, f].astype(f32) * inverse).astype(bf16)
-    for k in range(raw):
-
-        @pl.when(sent_raw(k))
-        def _():
-            scale_send(k).start()
-
-    def crosses(k):
-        late_far = 1 if k < half else 0
-        early_far = 1 if half <= k < n_sta - 2 else 0
-        return jnp.where(upper == 1, early_far, late_far) == 1
-
-    def white_send(k, wanted):
-        if k < raw:
-            wanted = jnp.logical_and(wanted, jnp.logical_not(sent_raw(k)))
-
-        @pl.when(wanted)
-        def _():
-            await_entry(k)
-            block_send(k, white)
-
-    for k in range(n_sta - 1):
-        if paired:
-            white_send(k, jnp.logical_or(prompt, jnp.logical_not(crosses(k))))
-        else:
-            white_send(k, True)
-
-    for f in range(fb):
-        for c in range(2):
-            blocks[me, c, f] = white[c, first_me + f]
-    if extra:
-
-        @pl.when(long_me)
-        def _():
-            for f in range(fb, most):
-                for c in range(2):
-                    blocks[me, c, f] = white[c, first_me + f]
-
-    if extra:
-        lax.fori_loop(fb * n_sta, bins_me * n_sta, table_step, 0)
     product[...] = jnp.zeros_like(product)
     slow_copy.wait()
     sx = slowness[0:1, :] + 32
@@ -424,6 +375,55 @@
     keep[...] = jnp.where(ids == row, norm, 0.0)
 
 
+    if n_bins > 1:
+        squares_of(n_bins - 1).wait_recv()
+    total = squares[0]
+    for b in range(1, n_bins):
+        total = total + squares[b]
+    inverse = 1.0 / jnp.sqrt(total / (2 * bins_dev * n_bins) + epsilon)
+    scales[me] = inverse
+    for f in range(bins_dev):
+        for c in range(2):
+            white[c, f] = (own[c, f].astype(f32) * inverse).astype(bf16)
+    for k in range(raw):
+
+        @pl.when(sent_raw(k))
+        def _():
+            scale_send(k).start()
+
+    def crosses(k):
+        late_far = 1 if k < half else 0
+        early_far = 1 if half <= k < n_sta - 2 else 0
+        return jnp.where(upper == 1, early_far, late_far) == 1
+
+    def white_send(k, wanted):
+        if k < raw:
+            wanted = jnp.logical_and(wanted, jnp.logical_not(sent_raw(k)))
+
+        @pl.when(wanted)
+        def _():
+            await_entry(k)
+            block_send(k, white)
+
+    for k in range(n_sta - 1):
+        if paired:
+            white_send(k, jnp.logical_or(prompt, jnp.logical_not(crosses(k))))
+        else:
+            white_send(k, True)
+
+    for f in range(fb):
+        for c in range(2):
+            blocks[me, c, f] = white[c, first_me + f]
+    if extra:
+
+        @pl.when(long_me)
+        def _():
+            for f in range(fb, most):
+                for c in range(2):
+                    blocks[me, c, f] = white[c, first_me + f]
+
+    if extra:
+        lax.fori_loop(fb * n_sta, bins_me * n_sta, table_step, 0)
     def turn(begin, end):
         def turn_step(step, carry):
             at = pl.ds(pl.multiple_of(step * sta_dev, sta_dev), sta_dev)

time: 19 us -> 19.2 us (1.011)
  no operation moved by 1% of the time
where the time goes in v4:
time: 19.2 us; the launch traced here: 19 us
  Pallas kernels  18.4 us (96%)
  local copies, waits for them, and re-layouts  0.62 us (3%)
    pallas_call x1, Pallas kernels, local(): pl.pallas_call(functools.partial(kernel, dims), out_shape=pltpu.VMEM((bin...  18.4 us
    unnamed x1, local copies, waits for them, and re-layouts  0.62 us

profile of v4, /device:TPU:0, one launch (start us, length us, event | category | flops | bytes accessed | tf_op | source)
XLA Modules:
  0.0 19.0 jit_solution(13302469808301499576)
XLA Ops:
  0.0 18.4 %beam_power.1 = f32[32,256]{1,0:T(8,128)S(1)} custom-call(bf16[2,32,8,256]{3,2,1,0:T(8,128)(2,1)} %spectra.1, s32[2,2048]{1,0:T(2,128)} %coords_hbm.1, s32[2,2048]{1,0:T(2,128)} %slowness_hbm.1), custom_call_target="tpu_custom_call" | custom-call | tf_op jit(solution)/shard_map/beam_power/pallas_call | solution.py:634
  18.4 0.6 %copy.5 = f32[32,256]{1,0:T(8,128)} copy(f32[32,256]{1,0:T(8,128)S(1)} %beam_power.1) | data formatting | bytes 65536
